TPU v7x, 32 devices: a whole 2x2x4 slice. The times are simulated.
32 devices in a mesh: row: 4 (over y, x), col: 8 (over z, core).
Axes of the slice: x: 2, y: 2, z: 4, core: 2. Of those that a mesh axis runs over, the one named last changes fastest.
Arguments:
- activations: bfloat16 [1024, 9216], P('col', 'row'), may hold values from -64 to 64
- output_grads: bfloat16 [1024, 73728], P('row', 'col'), may hold values from -16 to 16
- weight: bfloat16 [9216, 73728], P('row', 'col'), may hold values from -1 to 1
- row_moment: float32 [9216], P('row'), may hold values from 0.01 to 0.3
- col_moment: float32 [73728], P('col'), may hold values from 0.01 to 0.3
Outputs:
- new_weight: bfloat16 [9216, 73728], P('row', 'col')
- new_row: float32 [9216], P('row')
- new_col: float32 [73728], P('col')
All inputs are finite; a program needn't handle non-finite values.
Results may differ from a plain program's by a relative error of at most 0.0004.
Values may be sent and summed in bfloat16 or wider, within the bound.
No kernel may reach another device: no remote copies, remote signals or barrier semaphores. Data moves between devices by JAX's collectives and lax.ppermute only.
A program may use at most 256 MiB of HBM per device.

v0:
```python
import jax
import jax.numpy as jnp
from jax import lax
from jax.sharding import PartitionSpec as P

ADDED_SQUARE = 1e-30
DECAY_RATE = 0.8
CLIP_LIMIT = 1.0
STEP_SIZE = 0.1
MEAN_OFFSET = 1e-06


def on_device(activations, output_grads, weight, row_moment, col_moment):
    tile_rows, tile_cols = weight.shape
    total_rows = tile_rows * lax.axis_size("row")
    total_cols = tile_cols * lax.axis_size("col")
    entries = float(total_rows * total_cols)
    weight_wide = weight.astype(jnp.float32)
    weight_local = jnp.sum(weight_wide * weight_wide)
    weight_total = lax.psum(weight_local, ("row", "col"))
    contract = (((0,), (0,)), ((), ()))
    acts_all = lax.all_gather(activations, "col", axis=0, tiled=True)
    gradient = lax.dot_general(
        acts_all,
        lax.all_gather(output_grads, "row", axis=0, tiled=True),
        contract,
        preferred_element_type=jnp.float32,
    )
    squared = gradient * gradient
    row_part = jnp.sum(squared + ADDED_SQUARE, axis=1)
    col_part = jnp.sum(squared + ADDED_SQUARE, axis=0)
    row_total = lax.psum(row_part, "col")
    col_total = lax.psum(col_part, "row")
    new_row = DECAY_RATE * row_moment + (1.0 - DECAY_RATE) * row_total / total_cols
    new_col = DECAY_RATE * col_moment + (1.0 - DECAY_RATE) * col_total / total_rows
    inverse = lax.rsqrt(new_row[:, None] * new_col[None, :])
    ratio_local = jnp.sum(squared * inverse * inverse)
    leader = (lax.axis_index("col") == 0).astype(jnp.float32)
    row_local = leader * jnp.sum(new_row)
    row_sum, ratio_sum = lax.psum((row_local, ratio_local), ("row", "col"))
    row_mean = row_sum / total_rows
    rms_update = jnp.sqrt(row_mean * ratio_sum / entries)
    clip_factor = jnp.maximum(1.0, rms_update / CLIP_LIMIT)
    step_scale = STEP_SIZE * jnp.sqrt(weight_total / entries + MEAN_OFFSET)
    update = gradient * inverse * jnp.sqrt(row_mean)
    new_weight = (weight_wide - step_scale / clip_factor * update).astype(jnp.bfloat16)
    return (new_weight, new_row, new_col)


def solution(mesh):
    return jax.shard_map(
        on_device,
        mesh=mesh,
        in_specs=(P("col", "row"), P("row", "col"), P("row", "col"), P("row"), P("col")),
        out_specs=(P("row", "col"), P("row"), P("col")),
        check_vma=False,
    )
```

profile of v0, /device:TPU:12, one launch (start us, length us, event | category | flops | bytes accessed | tf_op | source)
XLA Modules:
  0.0 471.2 jit_solution(5277439258976595096)
XLA Ops:
  7.2 0.0 all-gather.3.cloned.1.call-start
  7.2 0.7 all-gather.3.cloned.1.call-update
  7.9 0.0 all-gather.5.cloned.1.call-start
  7.9 0.7 all-gather.5.cloned.1.call-update
  8.7 24.5 %fusion = f32[]{:T(128)} fusion(bf16[2304,9216]{1,0:T(8,128)(2,1)} %param.7), kind=kLoop, calls=%fused_computation.3 | loop fusion | flops 63700992 | bytes 42467332 | tf_op jit(solution)/shard_map/reduce_sum | solution.py:19
  33.1 0.0 copy-start.2
  33.2 0.0 copy-start.3
  33.2 27.4 %all-gather.3.cloned.1.call-done = bf16[1024,2304]{1,0:T(8,128)(2,1)} async-done(((bf16[128,2304]{1,0:T(8,128)(2,1)}), bf16[1024,2304]{1,0:T(8,128)(2,1)}) %all-gather.3.cloned.1.call-update) | async-done | bytes 4718608 | tf_op jit(solution)/shard_map/all_gather | solution.py:22
  60.5 177.9 %all-gather.5.cloned.1.call-done = bf16[1024,9216]{1,0:T(8,128)(2,1)} async-done(((bf16[256,9216]{1,0:T(8,128)(2,1)}), bf16[1024,9216]{1,0:T(8,128)(2,1)}) %all-gather.5.cloned.1.call-update) | async-done | bytes 18874384 | tf_op jit(solution)/shard_map/all_gather | solution.py:25
  238.4 59.5 %add_reduce_fusion = (f32[9216]{0:T(1024)S(1)}, f32[2304]{0:T(1024)S(1)}, f32[2304,9216]{1,0:T(8,128)}) fusion(bf16[1024,2304]{1,0:T(8,128)(2,1)} %all-gather.3.cloned.1.call-done, bf16[1024,9216]{1,0:T(8,128)(2,1)} %all-gather.5.cloned.1.call-done), kind=kOutput, calls=%fused_computation.7 | convolution fusion | flops 43571466240 | bytes 108573696 | tf_op jit(solution)/shard_map/dot_general | solution.py:23
  297.9 15.7 %psum.38 = f32[9216]{0:T(1024)S(1)} all-reduce(f32[9216]{0:T(1024)S(1)} %get-tuple-element.3), channel_id=1, replica_groups=mesh['row'=4,'col'=8] {'row'}, use_global_device_ids=true, to_apply=%region_7.0 | all-reduce | flops 9216 | bytes 73728 | tf_op jit(solution)/shard_map/psum | solution.py:33
  313.6 22.4 %psum.36 = f32[2304]{0:T(1024)S(1)} all-reduce(f32[2304]{0:T(1024)S(1)} %get-tuple-element.4), channel_id=1, replica_groups=mesh['row'=4,'col'=8] {'col'}, use_global_device_ids=true, to_apply=%region_3.0 | all-reduce | flops 2304 | bytes 18432 | tf_op jit(solution)/shard_map/psum | solution.py:32
  336.0 0.0 copy-done.2
  336.0 0.0 copy-done.3
  336.0 0.0 copy-start
  336.0 0.6 fusion.3
  336.6 0.0 copy-start.1
  336.6 28.1 %fusion.2 = f32[]{:T(128)} fusion(f32[2304,9216]{1,0:T(8,128)} %get-tuple-element.10, f32[9216]{0:T(1024)S(1)} %multiply_add_fusion, f32[2304]{0:T(1024)S(1)} %get-tuple-element.9), kind=kLoop, calls=%fused_computation.5 | loop fusion | flops 106168320 | bytes 84980736 | tf_op jit(solution)/shard_map/reduce_sum | solution.py:37
  365.4 43.2 %all-reduce = (f32[]{:T(128)}, f32[]{:T(128)}, f32[]{:T(128)}) all-reduce(f32[]{:T(128)S(6)} %mul.66, f32[]{:T(128)} %fusion, f32[]{:T(128)} %fusion.2), channel_id=1, replica_groups=mesh['row'=4,'col'=8] {'row','col'}, use_global_device_ids=true, to_apply=%region_5.0 | all-reduce | flops 3 | bytes 24 | tf_op jit(solution)/shard_map/psum | solution.py:40
  410.6 53.7 %fusion.1 = bf16[2304,9216]{1,0:T(8,128)(2,1)} fusion(bf16[2304,9216]{1,0:T(8,128)(2,1)} %param.7, f32[2304,9216]{1,0:T(8,128)} %get-tuple-element.10, f32[]{:T(128)S(6)} %sqrt.11, f32[]{:T(128)S(6)} %div.32, f32[9216]{0:T(1024)S(1)} %multiply_add_fusion, f32[2304]{0:T(1024)S(1)} %get-tuple-element.9), kind=kLoop, calls=%fused_computation.4 | loop fusion | flops 148635648 | bytes 169915392 | tf_op jit(solution)/shard_map/convert_element_type | solution.py:46
  464.3 0.0 copy-done
  464.3 0.0 copy-done.1
  (1 shorter events, 0.0 us)
Async XLA Ops:
  7.2 53.4 %all-gather.3.cloned.1.call-start = ((), (), s32[]{:S(2)}) async-start(), calls=%async_computation | async-start | bytes 5308416 | tf_op jit(solution)/shard_map/all_gather | solution.py:22
  7.9 230.5 %all-gather.5.cloned.1.call-start = ((), (), s32[]{:S(2)}) async-start(), calls=%async_computation.1 | async-start | bytes 23592960 | tf_op jit(solution)/shard_map/all_gather | solution.py:25
  33.1 302.8 %copy-start.2 = (f32[9216]{0:T(1024)S(1)}, f32[9216]{0:T(1024)}, u32[]{:S(2)}) copy-start(f32[9216]{0:T(1024)} %param.9) | copy-start | bytes 110596
  33.2 302.9 %copy-start.3 = (f32[2304]{0:T(1024)S(1)}, f32[2304]{0:T(1024)}, u32[]{:S(2)}) copy-start(f32[2304]{0:T(1024)} %param.8) | copy-start | bytes 27652
  336.0 128.3 %copy-start = (f32[9216]{0:T(1024)}, f32[9216]{0:T(1024)S(1)}, u32[]{:S(2)}) copy-start(f32[9216]{0:T(1024)S(1)} %multiply_add_fusion) | copy-start | bytes 110596
  336.6 127.7 %copy-start.1 = (f32[2304]{0:T(1024)}, f32[2304]{0:T(1024)S(1)}, u32[]{:S(2)}) copy-start(f32[2304]{0:T(1024)S(1)} %get-tuple-element.9) | copy-start | bytes 27652
Sparse Core Ops, SparseCore 0:
  9.6 50.8 all-gather.2
  62.4 175.9 all-gather.4
where the time goes:
time: 472 us; the launch traced here: 471 us
  waiting for transfers between devices  207 us (44%)
  other arithmetic  107 us (23%)
  blocking collectives  81.3 us (17%)
  matrix products  59.5 us (13%)
  between operations  16.8 us (4%)
    all_gather x1, waiting for transfers between devices, on_device(): lax.all_gather(output_grads, 'row', axis=0, tiled=True)  178 us
    dot_general x1, matrix products, on_device(): lax.dot_general(acts_all, lax.all_gather(output_grads, 'row', axis=0, til...  59.5 us
    convert_element_type x1, other arithmetic, on_device(): (weight_wide - step_scale / clip_factor * update).astype(jnp.bfloat16)  53.7 us
    psum x1, blocking collectives, on_device(): row_sum, ratio_sum = lax.psum((row_local, ratio_local), ('row', 'col'))  43.2 us
    reduce_sum x1, other arithmetic, on_device(): ratio_local = jnp.sum(squared * inverse * inverse)  28.1 us
    all_gather x1, waiting for transfers between devices, on_device(): acts_all = lax.all_gather(activations, 'col', axis=0, tiled=True)  27.4 us
    reduce_sum x1, other arithmetic, on_device(): weight_local = jnp.sum(weight_wide * weight_wide)  24.5 us
    psum x1, blocking collectives, on_device(): row_total = lax.psum(row_part, 'col')  22.4 us
  transfers between devices with their start and end apart: 2, of which 2 were waited for; matrix products, arithmetic and copies ran while one was open for 5% of the time, Pallas kernels for 0%

commit v1 on v0

--- a/solution.py
+++ b/solution.py
@@ -19,7 +19,12 @@
     weight_local = jnp.sum(weight_wide * weight_wide)
     weight_total = lax.psum(weight_local, ("row", "col"))
     contract = (((0,), (0,)), ((), ()))
-    acts_all = lax.all_gather(activations, "col", axis=0, tiled=True)
+    ring = [activations]
+    for hop in range(7):
+        ring.append(lax.ppermute(ring[-1], "col", [(dev, (dev + 1) % 8) for dev in range(8)]))
+    acts_all = jnp.roll(
+        jnp.concatenate(ring[::-1], axis=0), (lax.axis_index("col") + 1) * ring[0].shape[0], axis=0
+    )
     gradient = lax.dot_general(
         acts_all,
         lax.all_gather(output_grads, "row", axis=0, tiled=True),

time: 472 us -> 420 us (0.89)
  waiting for transfers between devices: 207 us -> 137 us
  local copies, waits for them, and re-layouts: 0.02 us -> 18.1 us
    all_gather x1, waiting for transfers between devices: 178 us -> 80 us  [on_device(): lax.all_gather(output_grads, 'row', axis=0, tiled=True)]
    ppermute x0 -> x7, waiting for transfers between devices: none -> 56.1 us  [on_device(): lax.ppermute(ring[-1], 'col', [(dev, (dev + 1) % 8) for dev in range(8)])]
    all_gather x1 -> x0, waiting for transfers between devices: 27.4 us -> none  [on_device(): acts_all = lax.all_gather(activations, 'col', axis=0, tiled=True)]
    unnamed x8 -> x25, local copies, waits for them, and re-layouts: 0.02 us -> 17.2 us
  transfers between devices with their start and end apart: 2 -> 8, of which waited for: 2 -> 7; matrix products, arithmetic and copies ran while one was open for 5% -> 10% of each run, Pallas kernels for 0% -> 0%
where the time goes in v1:
time: 420 us
  waiting for transfers between devices  137 us (33%)
  other arithmetic  107 us (25%)
  blocking collectives  81.5 us (19%)
  matrix products  59.5 us (14%)
  local copies, waits for them, and re-layouts  18.1 us (4%)
  between operations  16.8 us (4%)
    all_gather x1, waiting for transfers between devices, on_device(): lax.all_gather(output_grads, 'row', axis=0, tiled=True)  80 us
    dot_general x1, matrix products, on_device(): lax.dot_general(acts_all, lax.all_gather(output_grads, 'row', axis=0, til...  59.5 us
    ppermute x7, waiting for transfers between devices, on_device(): lax.ppermute(ring[-1], 'col', [(dev, (dev + 1) % 8) for dev in range(8)])  56.1 us
    convert_element_type x1, other arithmetic, on_device(): (weight_wide - step_scale / clip_factor * update).astype(jnp.bfloat16)  53.7 us
    psum x1, blocking collectives, on_device(): row_sum, ratio_sum = lax.psum((row_local, ratio_local), ('row', 'col'))  43.2 us
    reduce_sum x1, other arithmetic, on_device(): ratio_local = jnp.sum(squared * inverse * inverse)  28.1 us
    reduce_sum x1, other arithmetic, on_device(): weight_local = jnp.sum(weight_wide * weight_wide)  24.5 us
    psum x1, blocking collectives, on_device(): row_total = lax.psum(row_part, 'col')  22.6 us
  transfers between devices with their start and end apart: 8, of which 7 were waited for; matrix products, arithmetic and copies ran while one was open for 10% of the time, Pallas kernels for 0%

profile of v1, /device:TPU:12, one launch (start us, length us, event | category | flops | bytes accessed | tf_op | source)
XLA Modules:
  0.0 419.8 jit_solution(13385548711136100667)
XLA Ops:
  8.0 9.5 %collective-permute-done = bf16[128,2304]{1,0:T(8,128)(2,1)S(1)} collective-permute-done((bf16[128,2304]{1,0:T(8,128)(2,1)}, bf16[128,2304]{1,0:T(8,128)(2,1)S(1)}, u32[]{:S(2)}, u32[]{:S(2)}) %collective-permute-start) | collective-permute-done | bytes 589856 | tf_op jit(solution)/shard_map/ppermute | solution.py:24
  17.5 9.3 %collective-permute-done.1 = bf16[128,2304]{1,0:T(8,128)(2,1)S(1)} collective-permute-done((bf16[128,2304]{1,0:T(8,128)(2,1)S(1)}, bf16[128,2304]{1,0:T(8,128)(2,1)S(1)}, u32[]{:S(2)}, u32[]{:S(2)}) %collective-permute-start.1) | collective-permute-done | bytes 589856 | tf_op jit(solution)/shard_map/ppermute | solution.py:24
  26.8 9.3 %collective-permute-done.2 = bf16[128,2304]{1,0:T(8,128)(2,1)S(1)} collective-permute-done((bf16[128,2304]{1,0:T(8,128)(2,1)S(1)}, bf16[128,2304]{1,0:T(8,128)(2,1)S(1)}, u32[]{:S(2)}, u32[]{:S(2)}) %collective-permute-start.2) | collective-permute-done | bytes 589856 | tf_op jit(solution)/shard_map/ppermute | solution.py:24
  36.1 9.3 %collective-permute-done.3 = bf16[128,2304]{1,0:T(8,128)(2,1)S(1)} collective-permute-done((bf16[128,2304]{1,0:T(8,128)(2,1)S(1)}, bf16[128,2304]{1,0:T(8,128)(2,1)S(1)}, u32[]{:S(2)}, u32[]{:S(2)}) %collective-permute-start.3) | collective-permute-done | bytes 589856 | tf_op jit(solution)/shard_map/ppermute | solution.py:24
  45.4 9.3 %collective-permute-done.4 = bf16[128,2304]{1,0:T(8,128)(2,1)S(1)} collective-permute-done((bf16[128,2304]{1,0:T(8,128)(2,1)S(1)}, bf16[128,2304]{1,0:T(8,128)(2,1)S(1)}, u32[]{:S(2)}, u32[]{:S(2)}) %collective-permute-start.4) | collective-permute-done | bytes 589856 | tf_op jit(solution)/shard_map/ppermute | solution.py:24
  54.7 9.4 %collective-permute-done.5 = bf16[128,2304]{1,0:T(8,128)(2,1)} collective-permute-done((bf16[128,2304]{1,0:T(8,128)(2,1)S(1)}, bf16[128,2304]{1,0:T(8,128)(2,1)}, u32[]{:S(2)}, u32[]{:S(2)}) %collective-permute-start.5) | collective-permute-done | bytes 589856 | tf_op jit(solution)/shard_map/ppermute | solution.py:24
  64.1 24.5 %fusion = f32[]{:T(128)} fusion(bf16[2304,9216]{1,0:T(8,128)(2,1)} %param.7), kind=kLoop, calls=%fused_computation.3 | loop fusion | flops 63700992 | bytes 42467332 | tf_op jit(solution)/shard_map/reduce_sum | solution.py:19
  88.7 2.1 constant_dynamic-update-slice_fusion.15
  90.8 1.9 constant_dynamic-update-slice_fusion.14
  93.5 0.9 constant_dynamic-update-slice_fusion.12
  94.4 0.9 constant_dynamic-update-slice_fusion.11
  95.2 0.9 constant_dynamic-update-slice_fusion.10
  96.1 0.9 constant_dynamic-update-slice_fusion.9
  96.9 0.9 constant_dynamic-update-slice_fusion.8
  97.8 1.9 constant_dynamic-update-slice_fusion.7
  99.7 1.9 constant_dynamic-update-slice_fusion.6
  101.6 0.9 constant_dynamic-update-slice_fusion.5
  106.7 80.0 %all-gather.2.cloned.1.call-done = bf16[1024,9216]{1,0:T(8,128)(2,1)} async-done(((bf16[256,9216]{1,0:T(8,128)(2,1)}), bf16[1024,9216]{1,0:T(8,128)(2,1)}) %all-gather.2.cloned.1.call-update) | async-done | bytes 18874384 | tf_op jit(solution)/shard_map/all_gather | solution.py:30
  186.8 59.5 %add_reduce_fusion = (f32[9216]{0:T(1024)S(1)}, f32[2304]{0:T(1024)S(1)}, f32[2304,9216]{1,0:T(8,128)}) fusion(bf16[1024,9216]{1,0:T(8,128)(2,1)} %all-gather.2.cloned.1.call-done, bf16[2048,2304]{1,0:T(8,128)(2,1)} %constant_dynamic-update-slice_fusion, s32[]{:T(128)S(6)} %select_n.14), kind=kOutput, calls=%fused_computation.7 | convolution fusion | flops 43571466240 | bytes 108573696 | tf_op jit(solution)/shard_map/dot_general | solution.py:28
  246.3 15.7 %psum.38 = f32[9216]{0:T(1024)S(1)} all-reduce(f32[9216]{0:T(1024)S(1)} %get-tuple-element.3), channel_id=1, replica_groups=mesh['row'=4,'col'=8] {'row'}, use_global_device_ids=true, to_apply=%region_7.8 | all-reduce | flops 9216 | bytes 73728 | tf_op jit(solution)/shard_map/psum | solution.py:38
  262.0 22.6 %psum.36 = f32[2304]{0:T(1024)S(1)} all-reduce(f32[2304]{0:T(1024)S(1)} %get-tuple-element.4), channel_id=1, replica_groups=mesh['row'=4,'col'=8] {'col'}, use_global_device_ids=true, to_apply=%region_3.4 | all-reduce | flops 2304 | bytes 18432 | tf_op jit(solution)/shard_map/psum | solution.py:37
  285.2 28.1 %fusion.2 = f32[]{:T(128)} fusion(f32[2304,9216]{1,0:T(8,128)} %get-tuple-element.10, f32[9216]{0:T(1024)S(1)} %multiply_add_fusion, f32[2304]{0:T(1024)S(1)} %get-tuple-element.9), kind=kLoop, calls=%fused_computation.5 | loop fusion | flops 106168320 | bytes 84980736 | tf_op jit(solution)/shard_map/reduce_sum | solution.py:42
  313.9 43.2 %all-reduce = (f32[]{:T(128)}, f32[]{:T(128)}, f32[]{:T(128)}) all-reduce(f32[]{:T(128)S(6)} %mul.70, f32[]{:T(128)} %fusion, f32[]{:T(128)} %fusion.2), channel_id=1, replica_groups=mesh['row'=4,'col'=8] {'row','col'}, use_global_device_ids=true, to_apply=%region_5.6 | all-reduce | flops 3 | bytes 24 | tf_op jit(solution)/shard_map/psum | solution.py:45
  359.2 53.7 %fusion.1 = bf16[2304,9216]{1,0:T(8,128)(2,1)} fusion(bf16[2304,9216]{1,0:T(8,128)(2,1)} %param.7, f32[2304,9216]{1,0:T(8,128)} %get-tuple-element.10, f32[]{:T(128)S(6)} %sqrt.11, f32[]{:T(128)S(6)} %div.32, f32[9216]{0:T(1024)S(1)} %multiply_add_fusion, f32[2304]{0:T(1024)S(1)} %get-tuple-element.9), kind=kLoop, calls=%fused_computation.4 | loop fusion | flops 148635648 | bytes 169915392 | tf_op jit(solution)/shard_map/convert_element_type | solution.py:51
  (28 shorter events, 6.5 us)
Async XLA Ops:
  7.2 179.6 %all-gather.2.cloned.1.call-start = ((), (), s32[]{:S(2)}) async-start(), calls=%async_computation | async-start | bytes 23592960 | tf_op jit(solution)/shard_map/all_gather | solution.py:30
  7.9 89.0 %copy-start = (bf16[128,2304]{1,0:T(8,128)(2,1)S(1)}, bf16[128,2304]{1,0:T(8,128)(2,1)}, u32[]{:S(2)}) copy-start(bf16[128,2304]{1,0:T(8,128)(2,1)} %param.5) | copy-start | bytes 1769476
  7.9 9.6 %collective-permute-start = (bf16[128,2304]{1,0:T(8,128)(2,1)}, bf16[128,2304]{1,0:T(8,128)(2,1)S(1)}, u32[]{:S(2)}, u32[]{:S(2)}) collective-permute-start(bf16[128,2304]{1,0:T(8,128)(2,1)} %param.5), channel_id=1, source_target_pairs={{0,1},{1,2},{2,3},{3,4},{4,5},{5,6},{6,7},{7,0},{8,9},{9,10},{10,1... | collective-permute-start | bytes 1769480 | tf_op jit(solution)/shard_map/ppermute | solution.py:24
  17.5 9.3 %collective-permute-start.1 = (bf16[128,2304]{1,0:T(8,128)(2,1)S(1)}, bf16[128,2304]{1,0:T(8,128)(2,1)S(1)}, u32[]{:S(2)}, u32[]{:S(2)}) collective-permute-start(bf16[128,2304]{1,0:T(8,128)(2,1)S(1)} %collective-permute-done), channel_id=1, source_target_pairs={{0,1},{1,2},{2,3},{3,4},{4,5},{5,6},{6,7},{7,0},{8,9},{9,10},{10,1... | collective-permute-start | bytes 1769480 | tf_op jit(solution)/shard_map/ppermute | solution.py:24
  26.8 9.3 %collective-permute-start.2 = (bf16[128,2304]{1,0:T(8,128)(2,1)S(1)}, bf16[128,2304]{1,0:T(8,128)(2,1)S(1)}, u32[]{:S(2)}, u32[]{:S(2)}) collective-permute-start(bf16[128,2304]{1,0:T(8,128)(2,1)S(1)} %collective-permute-done.1), channel_id=1, source_target_pairs={{0,1},{1,2},{2,3},{3,4},{4,5},{5,6},{6,7},{7,0},{8,9},{9,10},{10,1... | collective-permute-start | bytes 1769480 | tf_op jit(solution)/shard_map/ppermute | solution.py:24
  36.1 9.3 %collective-permute-start.3 = (bf16[128,2304]{1,0:T(8,128)(2,1)S(1)}, bf16[128,2304]{1,0:T(8,128)(2,1)S(1)}, u32[]{:S(2)}, u32[]{:S(2)}) collective-permute-start(bf16[128,2304]{1,0:T(8,128)(2,1)S(1)} %collective-permute-done.2), channel_id=1, source_target_pairs={{0,1},{1,2},{2,3},{3,4},{4,5},{5,6},{6,7},{7,0},{8,9},{9,10},{10,1... | collective-permute-start | bytes 1769480 | tf_op jit(solution)/shard_map/ppermute | solution.py:24
  45.4 9.3 %collective-permute-start.4 = (bf16[128,2304]{1,0:T(8,128)(2,1)S(1)}, bf16[128,2304]{1,0:T(8,128)(2,1)S(1)}, u32[]{:S(2)}, u32[]{:S(2)}) collective-permute-start(bf16[128,2304]{1,0:T(8,128)(2,1)S(1)} %collective-permute-done.3), channel_id=1, source_target_pairs={{0,1},{1,2},{2,3},{3,4},{4,5},{5,6},{6,7},{7,0},{8,9},{9,10},{10,1... | collective-permute-start | bytes 1769480 | tf_op jit(solution)/shard_map/ppermute | solution.py:24
  54.7 9.4 %collective-permute-start.5 = (bf16[128,2304]{1,0:T(8,128)(2,1)S(1)}, bf16[128,2304]{1,0:T(8,128)(2,1)}, u32[]{:S(2)}, u32[]{:S(2)}) collective-permute-start(bf16[128,2304]{1,0:T(8,128)(2,1)S(1)} %collective-permute-done.4), channel_id=1, source_target_pairs={{0,1},{1,2},{2,3},{3,4},{4,5},{5,6},{6,7},{7,0},{8,9},{9,10},{10,1... | collective-permute-start | bytes 1769480 | tf_op jit(solution)/shard_map/ppermute | solution.py:24
  64.1 24.5 %collective-permute-start.6 = (bf16[128,2304]{1,0:T(8,128)(2,1)}, bf16[128,2304]{1,0:T(8,128)(2,1)}, u32[]{:S(2)}, u32[]{:S(2)}) collective-permute-start(bf16[128,2304]{1,0:T(8,128)(2,1)} %collective-permute-done.5), channel_id=1, source_target_pairs={{0,1},{1,2},{2,3},{3,4},{4,5},{5,6},{6,7},{7,0},{8,9},{9,10},{10,1... | collective-permute-start | bytes 1769480 | tf_op jit(solution)/shard_map/ppermute | solution.py:24
  106.7 177.8 %copy-start.3 = (f32[9216]{0:T(1024)S(1)}, f32[9216]{0:T(1024)}, u32[]{:S(2)}) copy-start(f32[9216]{0:T(1024)} %param.9) | copy-start | bytes 110596
  106.7 177.8 %copy-start.4 = (f32[2304]{0:T(1024)S(1)}, f32[2304]{0:T(1024)}, u32[]{:S(2)}) copy-start(f32[2304]{0:T(1024)} %param.8) | copy-start | bytes 27652
  284.6 74.6 %copy-start.1 = (f32[9216]{0:T(1024)}, f32[9216]{0:T(1024)S(1)}, u32[]{:S(2)}) copy-start(f32[9216]{0:T(1024)S(1)} %multiply_add_fusion) | copy-start | bytes 110596
  285.2 74.0 %copy-start.2 = (f32[2304]{0:T(1024)}, f32[2304]{0:T(1024)S(1)}, u32[]{:S(2)}) copy-start(f32[2304]{0:T(1024)S(1)} %get-tuple-element.9) | copy-start | bytes 27652
Sparse Core Ops, SparseCore 0:
  9.8 176.9 all-gather.1
